TPU v7x, 32 devices: a whole 2x2x4 slice. The times are simulated.
32 devices in a mesh: slab: 2 (over x), py: 4 (over y, core), px: 4 (over z).
Axes of the slice: x: 2, y: 2, z: 4, core: 2. Of those that a mesh axis runs over, the one named last changes fastest.
Arguments:
- state: bfloat16 [2, 3, 16, 1024, 1024], P(None, None, 'slab', ('py', 'px')), may hold values from -12 to 12
- shells: int32 [16, 1024, 1024], P('slab', ('py', 'px')), may hold values from 0 to 511
Outputs:
- restored: float32 [2, 3, 16, 1024, 1024], P(None, None, ('slab', 'py'), None, 'px')
- spectrum: float32 [512], replicated
All inputs are finite; a program needn't handle non-finite values.
Results may differ from a plain program's by a relative error of at most 0.0003.
Values may be sent and summed in bfloat16 or wider, within the bound.
A program may use at most 128 MiB of HBM per device.

v0:
```python
import math

import jax
import jax.numpy as jnp
from jax import lax
from jax.sharding import PartitionSpec as P

SHELLS = 512


def mode_energy(values):
    return 0.5 * jnp.sum(values * values, axis=(0, 1))


def bin_energy(energy, labels_in):
    flat_energy = energy.reshape(-1)
    flat_labels = labels_in.reshape(-1)
    mode_count = flat_energy.shape[0]
    block_len = math.gcd(mode_count, 16384)
    high_rows = SHELLS // 128
    energy_blocks = flat_energy.reshape(mode_count // block_len, block_len)
    label_blocks = flat_labels.reshape(mode_count // block_len, block_len)

    def add_block(running, pieces):
        values, labels = pieces
        upper = values.astype(jnp.bfloat16)
        remain = values - upper.astype(jnp.float32)
        middle = remain.astype(jnp.bfloat16)
        lower = (remain - middle.astype(jnp.float32)).astype(jnp.bfloat16)
        high_part = labels // 128
        low_part = labels % 128
        high_hot = (high_part[:, None] == jnp.arange(high_rows, dtype=jnp.int32)[None, :]).astype(
            jnp.bfloat16
        )
        weighted = jnp.concatenate(
            [high_hot * upper[:, None], high_hot * middle[:, None], high_hot * lower[:, None]],
            axis=1,
        )
        onehot = (low_part[:, None] == jnp.arange(128, dtype=jnp.int32)[None, :]).astype(
            jnp.bfloat16
        )
        partial_sum = lax.dot_general(
            weighted, onehot, (((0,), (0,)), ((), ())), preferred_element_type=jnp.float32
        )
        partial_sum = partial_sum.reshape(3, high_rows, 128)
        return (running + (partial_sum[0] + partial_sum[1] + partial_sum[2]), None)

    running, _ = lax.scan(
        add_block, jnp.zeros((high_rows, 128), jnp.float32), (energy_blocks, label_blocks)
    )
    return running.reshape(SHELLS)


def local(state, shells):
    py_count = lax.axis_size("py")
    px_count = lax.axis_size("px")
    planes = state.shape[2]
    rows_local = state.shape[3]
    columns = state.shape[4]
    planes_out = planes // py_count
    columns_out = columns // px_count
    sectioned = state.reshape(2, 3, planes, 1, 1, rows_local, columns)
    received = lax.all_to_all(
        lax.all_to_all(sectioned, "py", split_axis=2, concat_axis=3, tiled=True),
        "px",
        split_axis=6,
        concat_axis=4,
        tiled=True,
    )
    restored = received.reshape(
        2, 3, planes_out, rows_local * py_count * px_count, columns_out
    ).astype(jnp.float32)
    totals = bin_energy(mode_energy(state.astype(jnp.float32)), shells)
    modes_all = planes * rows_local * columns * lax.axis_size("slab") * py_count * px_count
    totals = lax.psum(totals, ("slab", "py", "px"))
    spectrum = totals * (SHELLS / modes_all)
    return (restored, spectrum)


def solution(mesh):
    return jax.shard_map(
        local,
        mesh=mesh,
        in_specs=(P(None, None, "slab", ("py", "px"), None), P("slab", ("py", "px"), None)),
        out_specs=(P(None, None, ("slab", "py"), None, "px"), P()),
        check_vma=False,
    )
```

profile of v0, /device:TPU:0, one launch (start us, length us, event | category | flops | bytes accessed | tf_op | source)
XLA Modules:
  0.0 352.4 jit_solution(16731340654529815363)
XLA Ops:
  0.6 6.7 %copy.16 = bf16[2,3,8,64,1024]{4,3,1,0,2:T(8,128)(2,1)} copy(bf16[2,3,8,64,1024]{4,3,2,1,0:T(8,128)(2,1)} %param.4) | data formatting | bytes 12582912 | tf_op args[0]
  7.4 5.3 %all-to-all-start = ((bf16[2,3,8,1,1,64,1024]{6,5,1,0,4,3,2:T(8,128)(2,1)}), bf16[2,3,8,1,1,64,1024]{6,5,1,0,4,3,2:T(8,128)(2,1)}, u32[]{:S(2)}, u32[]{:S(2)}) async-start(bf16[2,3,8,1,1,64,1024]{6,5,1,0,4,3,2:T(8,128)(2,1)} %bitcast.24), calls=%async_computation | async-start | bytes 12582912 | tf_op jit(solution)/shard_map/all_to_all | solution.py:64
  12.6 4.6 %multiply_reduce_fusion = f32[8,64,1024]{2,1,0:T(8,128)S(1)} fusion(bf16[2,3,8,64,1024]{4,3,2,1,0:T(8,128)(2,1)} %param.4), kind=kLoop, calls=%fused_computation.29 | loop fusion | flops 8912896 | bytes 8388608 | tf_op jit(solution)/shard_map/reduce_sum | solution.py:12
  20.7 63.3 %all-to-all-done = bf16[2,3,8,1,1,64,1024]{6,5,1,0,4,3,2:T(8,128)(2,1)} async-done(((bf16[2,3,8,1,1,64,1024]{6,5,1,0,4,3,2:T(8,128)(2,1)}), bf16[2,3,8,1,1,64,1024]{6,5,1,0,4,3,2:T(8,128)(2,1)}, u32[]{:S(2)}, u32[]{:S(2)}) %all-to-all-start) | async-done | bytes 6291488 | tf_op jit(solution)/shard_map/all_to_all | solution.py:64
  84.0 20.1 %copy.12 = bf16[2,3,4,2,1,1,64,1024]{6,2,3,1,0,7,5,4:T(4,128)(2,1)} copy(bf16[2,3,4,2,1,1,64,1024]{7,6,1,0,3,2,5,4:T(8,128)(2,1)} %bitcast.1) | data formatting | bytes 12582912 | tf_op jit(solution)/shard_map/all_to_all | solution.py:64
  104.1 10.9 %bitcast_bitcast_fusion = bf16[1024,1,2,3,2,4,64]{6,5,4,3,2,1,0:T(4,128)(2,1)} fusion(bf16[2,3,4,2,1,1,64,1024]{6,2,3,1,0,7,5,4:T(4,128)(2,1)} %copy.12), kind=kLoop, calls=%fused_computation.33 | loop fusion | bytes 12582912
  115.0 12.8 %reshape.115 = bf16[4,2,393216]{2,1,0:T(2,128)(2,1)} reshape(bf16[1024,1,2,3,2,4,64]{6,5,4,3,2,1,0:T(4,128)(2,1)} %bitcast_bitcast_fusion) | data formatting | bytes 12582912
  127.8 5.7 %all-to-all-start.1 = ((bf16[4,2,393216]{2,1,0:T(2,128)(2,1)}), bf16[4,2,393216]{2,1,0:T(2,128)(2,1)}, u32[]{:S(2)}, u32[]{:S(2)}) async-start(bf16[4,2,393216]{2,1,0:T(2,128)(2,1)} %reshape.115), calls=%async_computation.1 | async-start | bytes 12582912 | tf_op jit(solution)/shard_map/all_to_all | solution.py:63
  133.5 122.2 %while.13 = (s32[]{:T(128)}, f32[4,128]{1,0:T(4,128)S(1)}, s32[32,16384]{1,0:T(8,128)S(1)}, f32[32,16384]{1,0:T(8,128)}, s32[]{:T(128)}, /*index=5*/s32[]{:T(128)}) while((s32[]{:T(128)}, f32[4,128]{1,0:T(4,128)S(1)}, s32[32,16384]{1,0:T(8,128)S(1)}, f32[32,16384]{1,0:T(8,128)}, s32[]{:T(128)}, /*index=5*/s32[]{:T(128)}) %tuple.44), condition=%wide.region_2.3_spmd.clone, body=%wide.region_1.2_spmd.clone.sunk | while | flops 54315008 | bytes 1720407 | solution.py:48
  138.8 2.3 fusion.23
  142.6 2.3 fusion.23
  154.0 2.3 fusion.23
  157.9 2.3 fusion.23
  165.5 2.3 fusion.23
  169.3 2.3 fusion.23
  176.9 2.3 fusion.23
  180.8 2.3 fusion.23
  188.4 2.3 fusion.23
  192.2 2.3 fusion.23
  199.9 2.3 fusion.23
  203.7 2.3 fusion.23
  211.3 2.3 fusion.23
  215.1 2.3 fusion.23
  226.6 2.3 fusion.23
  230.4 2.3 fusion.23
  238.1 2.3 fusion.23
  241.9 2.3 fusion.23
  255.7 40.2 %psum.7 = f32[512]{0:T(512)S(1)} all-reduce(f32[512]{0:T(512)S(1)} %bitcast.29), channel_id=1, replica_groups=mesh['slab'=2,'py'=4,'px'=4] {'slab','py','px'}, use_global_device_ids=true, to_apply=%region_3.4 | all-reduce | flops 512 | bytes 4096 | tf_op jit(solution)/shard_map/psum | solution.py:75
  296.5 12.7 %reshape.116 = bf16[1024,1,2,3,2,4,64]{6,5,4,3,2,1,0:T(4,128)(2,1)} reshape(bf16[4,2,393216]{2,1,0:T(2,128)(2,1)} %all-to-all-done.1) | data formatting | bytes 12582912
  309.2 18.5 %copy.13 = bf16[2,3,2,4,1,64,1024]{6,5,4,3,2,1,0:T(8,128)(2,1)} copy(bf16[2,3,2,4,1,64,1024]{5,3,2,1,0,4,6:T(4,128)(2,1)} %bitcast.22) | data formatting | bytes 12582912 | tf_op jit(solution)/shard_map/all_to_all | solution.py:63
  327.7 12.6 %reshape.114 = f32[2,3,2,4,1,64,4,256]{7,6,5,3,2,1,0,4:T(4,128)} reshape(bf16[2,3,2,4,1,64,1024]{6,5,4,3,2,1,0:T(8,128)(2,1)} %copy.13) | data formatting | bytes 18874368 | tf_op jit(solution)/shard_map/convert_element_type | solution.py:72
  340.3 12.0 %copy.14 = f32[2,3,2,4,4,1,64,256]{7,6,4,3,2,1,0,5:T(8,128)} copy(f32[2,3,2,4,4,1,64,256]{7,4,6,3,2,1,0,5:T(4,128)} %bitcast.23) | data formatting | bytes 25165824 | tf_op jit(solution)/shard_map/convert_element_type | solution.py:72
  (244 shorter events, 82.2 us)
Async XLA Ops:
  7.4 76.6 %all-to-all-start = ((bf16[2,3,8,1,1,64,1024]{6,5,1,0,4,3,2:T(8,128)(2,1)}), bf16[2,3,8,1,1,64,1024]{6,5,1,0,4,3,2:T(8,128)(2,1)}, u32[]{:S(2)}, u32[]{:S(2)}) async-start(bf16[2,3,8,1,1,64,1024]{6,5,1,0,4,3,2:T(8,128)(2,1)} %bitcast.24), calls=%async_computation | async-start | bytes 12582912 | tf_op jit(solution)/shard_map/all_to_all | solution.py:64
  127.8 168.7 %all-to-all-start.1 = ((bf16[4,2,393216]{2,1,0:T(2,128)(2,1)}), bf16[4,2,393216]{2,1,0:T(2,128)(2,1)}, u32[]{:S(2)}, u32[]{:S(2)}) async-start(bf16[4,2,393216]{2,1,0:T(2,128)(2,1)} %reshape.115), calls=%async_computation.1 | async-start | bytes 12582912 | tf_op jit(solution)/shard_map/all_to_all | solution.py:63
where the time goes:
time: 356 us; the launch traced here: 352 us
  local copies, waits for them, and re-layouts  146 us (41%)
  matrix products  74.9 us (21%)
  waiting for transfers between devices  63.3 us (18%)
  blocking collectives  40.2 us (11%)
  other arithmetic  14 us (4%)
  starting transfers between devices  10.9 us (3%)
    dot_general x32, matrix products, add_block(): lax.dot_general(weighted, onehot, (((0,), (0,)), ((), ())), preferred_ele...  74.9 us
    all_to_all x1, waiting for transfers between devices, local(): lax.all_to_all(sectioned, 'py', split_axis=2, concat_axis=3, tiled=True)  63.3 us
    unnamed x4, local copies, waits for them, and re-layouts  43.1 us
    psum x1, blocking collectives, local(): totals = lax.psum(totals, ('slab', 'py', 'px'))  40.2 us
    dynamic_slice x64, local copies, waits for them, and re-layouts, bin_energy(): lax.scan(add_block, jnp.zeros((high_rows, 128), jnp.float32), (energy_blo...  36.7 us
    convert_element_type x2, local copies, waits for them, and re-layouts, local(): restored = received.reshape(2, 3, planes_out, rows_local * py_count * px_...  24.7 us
    all_to_all x1, local copies, waits for them, and re-layouts, local(): lax.all_to_all(sectioned, 'py', split_axis=2, concat_axis=3, tiled=True)  20.1 us
    all_to_all x1, local copies, waits for them, and re-layouts, local(): lax.all_to_all(lax.all_to_all(sectioned, 'py', split_axis=2, concat_axis=...  18.5 us
  transfers between devices with their start and end apart: 2, of which 1 were waited for; matrix products, arithmetic and copies ran while one was open for 37% of the time, Pallas kernels for 0%

commit v1 on v0

v1 whole, which is shorter than its diff:
```python
import functools

import jax
import jax.numpy as jnp
from jax import lax
from jax.experimental import pallas as pl
from jax.experimental.pallas import tpu as pltpu
from jax.sharding import PartitionSpec as P

SHELLS = 512
LOW = 32
HIGH = SHELLS // LOW
LANES = 128
SPEC_ROWS = SHELLS // LANES
GROUP_ROWS = 16
MESH = pl.DeviceIdType.MESH


def kernel(
    slab_count,
    py_count,
    px_count,
    state,
    shells,
    out,
    spec,
    modes,
    labels,
    slab_parts,
    group_parts,
    state_sem,
    label_sem,
    own_sem,
    send_sem,
    recv_sem,
    slab_send,
    slab_recv,
    part_send,
    part_recv,
):
    slab = lax.axis_index("slab")
    py = lax.axis_index("py")
    px = lax.axis_index("px")
    group = py_count * px_count
    me = py * px_count + px
    _, _, planes, rows, columns = state.shape
    planes_out = planes // py_count
    columns_out = columns // px_count

    def load_state(z):
        return pltpu.make_async_copy(state.at[:, :, z], modes.at[:, :, z], state_sem.at[z])

    def load_labels(z):
        return pltpu.make_async_copy(shells.at[z], labels.at[z], label_sem.at[z])

    def group_peer(step):
        peer = lax.rem(me + step, group)
        return (peer, peer // px_count, lax.rem(peer, px_count))

    def slab_peer(step):
        return lax.rem(slab + step, slab_count)

    def block(source, dest_py, dest_px):
        return source.at[
            :,
            :,
            pl.ds(dest_py * planes_out, planes_out),
            :,
            pl.ds(pl.multiple_of(dest_px * columns_out, columns_out), columns_out),
        ]

    def landing(source):
        return out.at[:, :, :, pl.ds(pl.multiple_of(source * rows, rows), rows), :]

    def send_block(dest_py, dest_px):
        return pltpu.make_async_remote_copy(
            src_ref=block(state, dest_py, dest_px),
            dst_ref=landing(me),
            send_sem=send_sem.at[dest_py * px_count + dest_px],
            recv_sem=recv_sem.at[me],
            device_id=(slab, dest_py, dest_px),
            device_id_type=MESH,
        )

    def take_block(source, source_py, source_px):
        return pltpu.make_async_remote_copy(
            src_ref=block(state, source_py, source_px),
            dst_ref=landing(source),
            send_sem=send_sem.at[source],
            recv_sem=recv_sem.at[source],
            device_id=(slab, source_py, source_px),
            device_id_type=MESH,
        )

    def send_at(distance):
        for turn in range(py_count):
            dest_py = lax.rem(py + turn, py_count)
            if distance == 0:
                if turn > 0:
                    send_block(dest_py, px).start()
                continue

            @pl.when(px + distance < px_count)
            def _():
                send_block(dest_py, px + distance).start()

            @pl.when(px - distance >= 0)
            def _():
                send_block(dest_py, px - distance).start()

    def slab_copy(dest, slot):
        return pltpu.make_async_remote_copy(
            src_ref=slab_parts.at[slab],
            dst_ref=slab_parts.at[slot],
            send_sem=slab_send.at[dest],
            recv_sem=slab_recv.at[slot],
            device_id=(dest, py, px),
            device_id_type=MESH,
        )

    def part_copy(dest, dest_py, dest_px, slot):
        return pltpu.make_async_remote_copy(
            src_ref=group_parts.at[me],
            dst_ref=group_parts.at[slot],
            send_sem=part_send.at[dest],
            recv_sem=part_recv.at[slot],
            device_id=(slab, dest_py, dest_px),
            device_id_type=MESH,
        )

    for z in range(planes):
        load_state(z).start()
        load_labels(z).start()

    barrier = pltpu.get_barrier_semaphore()
    for step in range(1, group):
        _, peer_py, peer_px = group_peer(step)
        pl.semaphore_signal(
            barrier, inc=1, device_id=(slab, peer_py, peer_px), device_id_type=MESH
        )
    for step in range(1, slab_count):
        pl.semaphore_signal(
            barrier, inc=1, device_id=(slab_peer(step), py, px), device_id_type=MESH
        )
    pl.semaphore_wait(barrier, group - 1 + slab_count - 1)

    for distance in range(px_count - 1):
        send_at(distance)

    low_ids = lax.broadcasted_iota(jnp.int32, (LOW, columns), 0)
    high_ids = lax.broadcasted_iota(jnp.int32, (HIGH, columns), 0)

    def add_rows(z, start, running):
        values = modes[:, :, z, pl.ds(start, GROUP_ROWS), :].astype(jnp.float32)
        energy = 0.5 * jnp.sum(values * values, axis=(0, 1))
        upper = energy.astype(jnp.bfloat16).astype(jnp.float32)
        lower = energy - upper
        numbers = labels[z, pl.ds(start, GROUP_ROWS), :]
        high = numbers >> (LOW.bit_length() - 1)
        low = numbers & (LOW - 1)
        for row in range(GROUP_ROWS):
            one = slice(row, row + 1)
            hot = high_ids == high[one]
            weighted = jnp.concatenate(
                [jnp.where(hot, upper[one], 0.0), jnp.where(hot, lower[one], 0.0)], axis=0
            ).astype(jnp.bfloat16)
            onehot = jnp.where(low_ids == low[one], 1.0, 0.0).astype(jnp.bfloat16)
            running = running + lax.dot_general(
                weighted, onehot, (((1,), (1,)), ((), ())), preferred_element_type=jnp.float32
            )
        return running

    running = jnp.zeros((2 * HIGH, LOW), jnp.float32)
    for z in range(planes):
        load_state(z).wait()
        load_labels(z).wait()

    own = pltpu.make_async_copy(block(modes, py, px), landing(me), own_sem)
    own.start()

    groups = rows // GROUP_ROWS
    running = lax.fori_loop(
        0,
        planes * groups,
        lambda i, total: add_rows(
            i // groups, pl.multiple_of(lax.rem(i, groups) * GROUP_ROWS, GROUP_ROWS), total
        ),
        running,
    )
    part = running[:HIGH] + running[HIGH:]
    per_row = LANES // LOW
    for high in range(HIGH):
        lane = (high % per_row) * LOW
        slab_parts[slab, high // per_row : high // per_row + 1, lane : lane + LOW] = part[
            high : high + 1
        ]

    for step in range(1, slab_count):
        slab_copy(slab_peer(step), slab).start()
    for step in range(1, slab_count):
        slab_copy(slab_peer(step), slab_peer(step)).wait_recv()
    total = slab_parts[0]
    for slot in range(1, slab_count):
        total = total + slab_parts[slot]
    group_parts[me] = total
    for step in range(1, group):
        part_copy(*group_peer(step), me).start()

    send_at(px_count - 1)

    for step in range(1, group):
        peer, peer_py, peer_px = group_peer(step)
        part_copy(peer, peer_py, peer_px, peer).wait_recv()
    total = group_parts[0]
    for slot in range(1, group):
        total = total + group_parts[slot]
    spec[...] = total

    own.wait()
    for step in range(1, slab_count):
        slab_copy(slab_peer(step), slab).wait_send()
    for step in range(1, group):
        peer, peer_py, peer_px = group_peer(step)
        part_copy(peer, peer_py, peer_px, me).wait_send()
        send_block(peer_py, peer_px).wait_send()
        take_block(peer, peer_py, peer_px).wait_recv()


def local(state, shells):
    slab_count = lax.axis_size("slab")
    py_count = lax.axis_size("py")
    px_count = lax.axis_size("px")
    group = py_count * px_count
    _, _, planes, rows, columns = state.shape
    moved, totals = pl.pallas_call(
        functools.partial(kernel, slab_count, py_count, px_count),
        out_shape=(
            jax.ShapeDtypeStruct(
                (2, 3, planes // py_count, rows * group, columns // px_count), state.dtype
            ),
            jax.ShapeDtypeStruct((SPEC_ROWS, LANES), jnp.float32),
        ),
        in_specs=[pl.BlockSpec(memory_space=pl.ANY)] * 2,
        out_specs=(
            pl.BlockSpec(memory_space=pl.ANY),
            pl.BlockSpec(memory_space=pltpu.VMEM),
        ),
        scratch_shapes=[
            pltpu.VMEM(state.shape, state.dtype),
            pltpu.VMEM(shells.shape, shells.dtype),
            pltpu.VMEM((slab_count, SPEC_ROWS, LANES), jnp.float32),
            pltpu.VMEM((group, SPEC_ROWS, LANES), jnp.float32),
            pltpu.SemaphoreType.DMA((planes,)),
            pltpu.SemaphoreType.DMA((planes,)),
            pltpu.SemaphoreType.DMA,
            pltpu.SemaphoreType.DMA((group,)),
            pltpu.SemaphoreType.DMA((group,)),
            pltpu.SemaphoreType.DMA((slab_count,)),
            pltpu.SemaphoreType.DMA((slab_count,)),
            pltpu.SemaphoreType.DMA((group,)),
            pltpu.SemaphoreType.DMA((group,)),
        ],
        compiler_params=pltpu.CompilerParams(collective_id=0, has_side_effects=True),
    )(state, shells)
    modes_all = planes * rows * columns * slab_count * group
    spectrum = totals.reshape(SHELLS) * (SHELLS / modes_all)
    return (moved.astype(jnp.float32), spectrum)


def solution(mesh):
    return jax.shard_map(
        local,
        mesh=mesh,
        in_specs=(P(None, None, "slab", ("py", "px"), None), P("slab", ("py", "px"), None)),
        out_specs=(P(None, None, ("slab", "py"), None, "px"), P()),
        check_vma=False,
    )
```

time: 356 us -> 162 us (0.46); the launches traced: 352 us -> 162 us
  Pallas kernels: 0 us -> 151 us
  local copies, waits for them, and re-layouts: 146 us -> 0 us
  matrix products: 74.9 us -> 0 us
  waiting for transfers between devices: 63.3 us -> 0 us
  blocking collectives: 40.2 us -> 0 us
  starting transfers between devices: 10.9 us -> 0 us
  other arithmetic: 14 us -> 10.1 us
    pallas_call x0 -> x1, Pallas kernels: none -> 151 us  [local(): pl.pallas_call(functools.partial(kernel, slab_count, py_count, px_count),...]
    dot_general x32 -> x0, matrix products: 74.9 us -> none  [add_block(): lax.dot_general(weighted, onehot, (((0,), (0,)), ((), ())), preferred_ele...]
    all_to_all x2 -> x0, waiting for transfers between devices: 63.3 us -> none  [the longest x1 63.3 us: local(): lax.all_to_all(sectioned, 'py', split_axis=2, concat_axis=3, tiled=True)]
    unnamed x4 -> x0, local copies, waits for them, and re-layouts: 43.1 us -> none
    psum x1 -> x0, blocking collectives: 40.2 us -> none  [local(): totals = lax.psum(totals, ('slab', 'py', 'px'))]
    all_to_all x2 -> x0, local copies, waits for them, and re-layouts: 38.7 us -> none  [the longest x1 20.1 us: local(): lax.all_to_all(sectioned, 'py', split_axis=2, concat_axis=3, tiled=True)]
    dynamic_slice x64 -> x0, local copies, waits for them, and re-layouts: 36.7 us -> none  [bin_energy(): lax.scan(add_block, jnp.zeros((high_rows, 128), jnp.float32), (energy_blo...]
    convert_element_type x2 -> x0, local copies, waits for them, and re-layouts: 24.7 us -> none  [local(): restored = received.reshape(2, 3, planes_out, rows_local * py_count * px_...]
  transfers between devices with their start and end apart: 2 -> 0, of which waited for: 1 -> 0; matrix products, arithmetic and copies ran while one was open for 37% -> 0% of each run, Pallas kernels for 0% -> 0%
where the time goes in v1:
time: 162 us
  Pallas kernels  151 us (93%)
  other arithmetic  10.1 us (6%)
    pallas_call x1, Pallas kernels, local(): pl.pallas_call(functools.partial(kernel, slab_count, py_count, px_count),...  151 us
    convert_element_type x1, other arithmetic, local(): return (moved.astype(jnp.float32), spectrum)  8.81 us

profile of v1, /device:TPU:0, one launch (start us, length us, event | category | flops | bytes accessed | tf_op | source)
XLA Modules:
  0.0 162.0 jit_solution(7160783633002826748)
XLA Ops:
  0.6 151.3 %shard_map.41 = (bf16[2,3,2,1024,256]{4,3,2,1,0:T(8,128)(2,1)}, f32[4,128]{1,0:T(4,128)}) custom-call(bf16[2,3,8,64,1024]{4,3,2,1,0:T(8,128)(2,1)} %state.1, s32[8,64,1024]{2,1,0:T(8,128)} %shells.1), custom_call_target="tpu_custom_call" | custom-call | tf_op jit(solution)/shard_map/pallas_call | solution.py:235
  151.9 1.3 multiply_bitcast_fusion
  153.2 8.8 %convert_element_type.3 = f32[2,3,2,1024,256]{4,3,2,1,0:T(8,128)} convert(bf16[2,3,2,1024,256]{4,3,2,1,0:T(8,128)(2,1)} %get-tuple-element.4) | non-fusion elementwise | flops 3145728 | bytes 18874368 | tf_op jit(solution)/shard_map/convert_element_type | solution.py:267

commit v2 on v1

--- a/solution.py
+++ b/solution.py
@@ -144,7 +144,7 @@
         )
     pl.semaphore_wait(barrier, group - 1 + slab_count - 1)
 
-    for distance in range(px_count - 1):
+    for distance in range(px_count - 1, 0, -1):
         send_at(distance)
 
     low_ids = lax.broadcasted_iota(jnp.int32, (LOW, columns), 0)
@@ -175,7 +175,7 @@
         load_state(z).wait()
         load_labels(z).wait()
 
-    own = pltpu.make_async_copy(block(modes, py, px), landing(me), own_sem)
+    own = pltpu.make_async_copy(block(state, py, px), landing(me), own_sem)
     own.start()
 
     groups = rows // GROUP_ROWS
@@ -206,7 +206,7 @@
     for step in range(1, group):
         part_copy(*group_peer(step), me).start()
 
-    send_at(px_count - 1)
+    send_at(0)
 
     for step in range(1, group):
         peer, peer_py, peer_px = group_peer(step)
@@ -235,14 +235,14 @@
     moved, totals = pl.pallas_call(
         functools.partial(kernel, slab_count, py_count, px_count),
         out_shape=(
-            jax.ShapeDtypeStruct(
+            pltpu.VMEM(
                 (2, 3, planes // py_count, rows * group, columns // px_count), state.dtype
             ),
             jax.ShapeDtypeStruct((SPEC_ROWS, LANES), jnp.float32),
         ),
         in_specs=[pl.BlockSpec(memory_space=pl.ANY)] * 2,
         out_specs=(
-            pl.BlockSpec(memory_space=pl.ANY),
+            pl.BlockSpec(memory_space=pltpu.VMEM),
             pl.BlockSpec(memory_space=pltpu.VMEM),
         ),
         scratch_shapes=[
@@ -260,8 +260,11 @@
             pltpu.SemaphoreType.DMA((group,)),
             pltpu.SemaphoreType.DMA((group,)),
         ],
-        compiler_params=pltpu.CompilerParams(collective_id=0, has_side_effects=True),
-    )(state, shells)
+        compiler_params=pltpu.CompilerParams(collective_id=0, has_side_effects=True, vmem_limit_bytes=24 << 20),
+    )(
+        pltpu.with_memory_space_constraint(state, pltpu.HBM),
+        pltpu.with_memory_space_constraint(shells, pltpu.HBM),
+    )
     modes_all = planes * rows * columns * slab_count * group
     spectrum = totals.reshape(SHELLS) * (SHELLS / modes_all)
     return (moved.astype(jnp.float32), spectrum)

time: 162 us -> 152 us (0.938)
  Pallas kernels: 151 us -> 145 us
  other arithmetic: 10.1 us -> 6.6 us
    pallas_call x1, Pallas kernels: 151 us -> 145 us  [local(): pl.pallas_call(functools.partial(kernel, slab_count, py_count, px_count),...]
    convert_element_type x1, other arithmetic: 8.81 us -> 6.02 us  [local(): return (moved.astype(jnp.float32), spectrum)]
where the time goes in v2:
time: 152 us
  Pallas kernels  145 us (95%)
  other arithmetic  6.6 us (4%)
    pallas_call x1, Pallas kernels, local(): pl.pallas_call(functools.partial(kernel, slab_count, py_count, px_count),...  145 us
    convert_element_type x1, other arithmetic, local(): return (moved.astype(jnp.float32), spectrum)  6.02 us

profile of v2, /device:TPU:0, one launch (start us, length us, event | category | flops | bytes accessed | tf_op | source)
XLA Modules:
  0.0 151.8 jit_solution(8669574692586738322)
XLA Ops:
  0.6 144.5 %shard_map.41 = (bf16[2,3,2,1024,256]{4,3,2,1,0:T(8,128)(2,1)S(1)}, f32[4,128]{1,0:T(4,128)S(1)}) custom-call(bf16[2,3,8,64,1024]{4,3,2,1,0:T(8,128)(2,1)} %state.1, s32[8,64,1024]{2,1,0:T(8,128)} %shells.1), custom_call_target="tpu_custom_call" | custom-call | tf_op jit(solution)/shard_map/pallas_call | solution.py:235
  145.2 0.6 multiply_bitcast_fusion
  145.8 6.0 %convert_element_type.3 = f32[2,3,2,1024,256]{4,3,2,1,0:T(8,128)} convert(bf16[2,3,2,1024,256]{4,3,2,1,0:T(8,128)(2,1)S(1)} %get-tuple-element.4) | non-fusion elementwise | flops 3145728 | bytes 18874368 | tf_op jit(solution)/shard_map/convert_element_type | solution.py:270
